TPU v7x, 8 devices: a whole 2x2x1 slice. The times are simulated.
8 devices in a mesh: dp: 2 (over z, y), ep: 4 (over x, core).
Axes of the slice: x: 2, y: 2, z: 1, core: 2. Of those that a mesh axis runs over, the one named last changes fastest.
Arguments:
- x_in: bfloat16 [1536, 2560], P(('dp', 'ep')), parts along dimension 0
- norm_gain: bfloat16 [2560], replicated
- w_router: bfloat16 [2560, 64], replicated
- expert_ids: int32 [1536, 6], P(('dp', 'ep')), parts along dimension 0
- w_gate: bfloat16 [64, 2560, 1536], P('ep')
- w_up: bfloat16 [64, 2560, 1536], P('ep')
- w_down: bfloat16 [64, 1536, 2560], P('ep')
Outputs:
- output: bfloat16 [1536, 2560], P(('dp', 'ep')), parts along dimension 0
There are 2 independent parts. A program takes and returns all parts, laid end to end along the dimension named above; an argument that names none is the same for every part.
All inputs are finite; a program needn't handle non-finite values.
Results may differ from a plain program's by a relative error of at most 0.001.
Values are sent between devices in bfloat16 or wider.
A program may use at most 1.5 GiB of HBM per device.

v0:
```python
import jax
import jax.numpy as jnp
from jax import lax
from jax.experimental import pallas as pl
from jax.experimental.pallas import tpu as pltpu
from jax.sharding import PartitionSpec as P

EPS = 1e-6
TOK = 192
PAD = 256
CAP = 36
PROW = 2 * CAP
GROW = 80
EROW = 4 * CAP
NE = 16
DSLOT = NE // 2 * PROW
MISS = -100.0
KC = 512
NK = 5
FF = 1536
NF = 3
NSLOT = 16
AHEAD = NSLOT // 2
G0, GS, G3 = 6, 3, 2
S1 = G0 * NK
S3 = S1 + 2 * GS * NK
P1 = S3 + G3 * NK
WC = 256
NC = NK * KC // WC
P2 = NC * NE // 4
f32, bf16, i32 = jnp.float32, jnp.bfloat16, jnp.int32
MESH = pl.DeviceIdType.MESH


def kernel(x_hbm, gain_hbm, wr_hbm, ids_hbm, wg_hbm, wu_hbm, wd_hbm, out_hbm,
           xv, gv, wrv, idv, h_all, pos_own, gate_own, pos_all, gate_all, gat, cmb, acc, act, ring, xg, xy, xp, sib, rem,
           in_sem, out_sem, ring_sem, h_send, h_recv, p_send, p_recv, g_send, g_recv, x_send, x_recv, a_send, a_recv,
           s_send, s_recv, r_send, r_recv):
    me = lax.axis_index("ep")
    dp = lax.axis_index("dp")
    chip = me // 2
    core = me % 2
    sibling = chip * 2 + (1 - core)
    partner = (1 - chip) * 2 + core
    diag = (1 - chip) * 2 + (1 - core)
    peers = (partner, diag, sibling)
    twin = {"dp": 1 - dp, "ep": me}

    ins = [pltpu.make_async_copy(s, d, in_sem.at[i]) for i, (s, d) in enumerate(
        ((ids_hbm, idv), (x_hbm, xv), (gain_hbm, gv), (wr_hbm, wrv)))]
    for i in (1, 2, 0, 3):
        ins[i].start()

    def slot_of(s, i):
        return (2 * s + i) % NSLOT

    def fill_up(s, e, k):
        for m, w in enumerate((wg_hbm, wu_hbm)):
            for n in range(NF):
                pltpu.make_async_copy(
                    w.at[e, pl.ds(k * KC, KC), pl.ds(n * KC, KC)],
                    ring.at[slot_of(s, m), pl.ds(n * KC, KC)], ring_sem.at[slot_of(s, m)]).start()

    def fill_first(s):
        fill_up(s, s % G0, s // G0)

    def fill_shared(s):
        t = s - S1
        g, u = t // (GS * NK), t % (GS * NK)
        i = u % GS
        fill_up(s, 6 + 2 * g + i + i // 2 * (4 - g + 2 * dp), u // GS)

    def fill_last(s):
        fill_up(s, 10 + (s - S3) % G3, (s - S3) // G3)

    def fill_down(s):
        p = s - P1
        c, q = p // (NE // 4), p % (NE // 4)
        for i in range(4):
            slot = slot_of(s, i // 2)
            pltpu.make_async_copy(
                wd_hbm.at[4 * q + i, :, pl.ds(pl.multiple_of(c * WC, WC), WC)],
                ring.at[slot, :, pl.ds(i % 2 * WC, WC)], ring_sem.at[slot]).start()

    spans = [(0, S1, fill_first), (S1, S3, fill_shared), (S3, P1, fill_last), (P1, P1 + P2, fill_down)]

    def fill(s, low, high):
        todo = [v for v in spans if v[0] <= high and low < v[1]]
        for a, b, fn in todo:
            if a <= low and high < b:
                fn(s)
            elif b <= low or high < a:
                pass
            else:
                pl.when((s >= a) & (s < b))(lambda fn=fn: fn(s))

    def wait_up(slot):
        pltpu.make_async_copy(wd_hbm.at[0, :, pl.ds(0, KC)], ring.at[slot], ring_sem.at[slot]).wait()

    barrier = pltpu.get_barrier_semaphore()
    for d in peers:
        pl.semaphore_signal(barrier, inc=1, device_id={"ep": d}, device_id_type=MESH)
    pl.semaphore_signal(barrier, inc=1, device_id=twin, device_id_type=MESH)

    for d in range(4):
        h_all[:, d * PAD + TOK:(d + 1) * PAD, :] = jnp.zeros((NK, PAD - TOK, KC), bf16)
    for d in range(4):
        pos_own[d] = jnp.full((NE, PAD), MISS, f32)
        gate_own[d] = jnp.zeros((NE, PAD), f32)

    for c in ins[1:3]:
        c.wait()
    for s in range(AHEAD):
        fill(s, s, s)
    my_rows = pl.ds(pl.multiple_of(me * PAD, PAD), TOK)
    ssq = jnp.zeros((TOK, 1), f32)
    for k in range(NK):
        xc = xv[:, k * KC:(k + 1) * KC].astype(f32)
        ssq = ssq + jnp.sum(xc * xc, axis=1, keepdims=True)
    gains = gv[...].astype(f32)
    inv = lax.rsqrt(ssq * (1.0 / (NK * KC)) + EPS)
    for k in range(NK):
        xc = xv[:, k * KC:(k + 1) * KC].astype(f32)
        gain = jnp.concatenate([gains[4 * k + i:4 * k + i + 1, :] for i in range(4)], axis=1)
        h_all[k, my_rows, :] = (xc * inv * gain).astype(bf16)

    pl.semaphore_wait(barrier, 4)

    def small_copy(own, everyone, ss, rs, idx):
        return pltpu.make_async_remote_copy(
            src_ref=own.at[peers[idx]], dst_ref=everyone.at[me], send_sem=ss.at[idx], recv_sem=rs.at[idx],
            device_id={"ep": peers[idx]}, device_id_type=MESH)

    def pos_copy(idx):
        return small_copy(pos_own, pos_all, p_send, p_recv, idx)

    def gate_copy(idx):
        return small_copy(gate_own, gate_all, g_send, g_recv, idx)

    def h_copy(k, owner, target, ss):
        rows = pl.ds(pl.multiple_of(owner * PAD, PAD), TOK)
        return pltpu.make_async_remote_copy(
            src_ref=h_all.at[k, rows], dst_ref=h_all.at[k, rows], send_sem=h_send.at[k, ss], recv_sem=h_recv.at[k, ss],
            device_id={"ep": target}, device_id_type=MESH)

    def own_to_sibling(k):
        return h_copy(k, me, sibling, 0)

    def own_to_partner(k):
        return h_copy(k, me, partner, 1)

    def hand_on(k):
        return h_copy(k, partner, sibling, 2)

    def x_copy(k, i):
        return pltpu.make_async_remote_copy(
            src_ref=xy.at[(k * 2 + 1 - dp) * 2 + i], dst_ref=xp.at[k, i], send_sem=x_send.at[k, i], recv_sem=x_recv.at[k, i],
            device_id=twin, device_id_type=MESH)

    def a_copy(i, n):
        return pltpu.make_async_remote_copy(
            src_ref=xy.at[(n * 2 + dp) * 2 + i], dst_ref=act.at[12 + 2 * dp + i, :, pl.ds(n * KC, KC)],
            send_sem=a_send.at[i, n], recv_sem=a_recv.at[i, n], device_id=twin, device_id_type=MESH)

    own_to_partner(0).start()
    own_to_sibling(0).start()
    ins[0].wait()
    e_iota = lax.broadcasted_iota(i32, (64, TOK), 0)
    hit = jnp.zeros((64, TOK), f32)
    for j in range(6):
        hit = hit + jnp.where(idv[j:j + 1, :] == e_iota, 1.0, 0.0)
    upper = (lax.broadcasted_iota(i32, (TOK, TOK), 0) < lax.broadcasted_iota(i32, (TOK, TOK), 1)).astype(f32).astype(bf16)
    before = jnp.dot(hit.astype(bf16), upper, preferred_element_type=f32)
    pos = jnp.where(hit > 0.5, before, MISS)
    for d in range(4):
        pos_own[d, :, 0:TOK] = pos[d * NE:(d + 1) * NE]

    for idx in range(3):
        pos_copy(idx).start()
    for k in range(1, NK):
        own_to_partner(k).start()
        own_to_sibling(k).start()

    ins[3].wait()
    logits = jnp.zeros((64, TOK), f32)
    for k in range(NK):
        logits = logits + lax.dot_general(
            wrv[:, k * KC:(k + 1) * KC], h_all[k, my_rows, :], (((1,), (1,)), ((), ())), preferred_element_type=f32)
    ex = jnp.exp(logits - jnp.max(logits, axis=0, keepdims=True))
    prob = ex / jnp.sum(ex, axis=0, keepdims=True)
    picked = prob * hit
    gates = picked / jnp.sum(picked, axis=0, keepdims=True)
    for d in range(4):
        gate_own[d, :, 0:TOK] = gates[d * NE:(d + 1) * NE]
    for idx in range(3):
        gate_copy(idx).start()
    pos_all[me] = pos_own[me]
    gate_all[me] = gate_own[me]

    own_to_partner(0).wait_recv()
    hand_on(0).start()

    for idx in range(3):
        pos_copy(idx).wait_recv()

    ri = lax.broadcasted_iota(i32, (GROW, PAD), 0)
    r_iota = ri.astype(f32)
    low = ri < CAP
    for d in range(4):
        for j in range(NE // 2):
            ea, eb = 2 * j + d % 2, 2 * j + 1 - d % 2
            want = jnp.where(low, pos_all[d, ea:ea + 1, :], pos_all[d, eb:eb + 1, :] + CAP)
            gat[d, j] = jnp.where(r_iota == want, 1.0, 0.0).astype(bf16)

    def build_combine():
        for idx in range(3):
            gate_copy(idx).wait_recv()
        le = lax.broadcasted_iota(i32, (NE, DSLOT), 1)
        ee = lax.broadcasted_iota(i32, (NE, DSLOT), 0)
        lane = lax.broadcasted_iota(i32, (TOK, DSLOT), 1) % PROW
        slot_r = jnp.where(lane < CAP, lane, lane - CAP).astype(f32)
        for d in range(4):
            swap = jnp.where(le % PROW < CAP, d % 2, 1 - d % 2)
            expand = (le // PROW * 2 + swap == ee).astype(f32).astype(bf16)
            ptok = jnp.transpose(pos_all[d])[:TOK]
            wtok = jnp.transpose(gate_all[d])[:TOK]
            pexp = jnp.dot(ptok.astype(bf16), expand, preferred_element_type=f32)
            sel = pexp == slot_r
            rest = wtok
            for i in range(3):
                part = rest.astype(bf16)
                rest = rest - part.astype(f32)
                wexp = jnp.dot(part, expand, preferred_element_type=f32)
                cmb[d, i] = jnp.where(sel, wexp, 0.0).astype(bf16)

    half = lax.broadcasted_iota(i32, (PROW, KC), 0) < CAP

    def gather(k, pair, n_pair, store):
        outs = [jnp.dot(gat[d, pl.ds(pair, n_pair)].reshape(n_pair * GROW, PAD),
                        h_all[k, d * PAD:(d + 1) * PAD, :], preferred_element_type=f32) for d in range(4)]
        for jj in range(n_pair):
            o = [v[jj * GROW:jj * GROW + PROW] for v in outs]
            store(jj, 0, jnp.concatenate(
                [jnp.where(half, o[0], o[1]), jnp.where(half, o[2], o[3])], axis=0).astype(bf16))
            store(jj, 1, jnp.concatenate(
                [jnp.where(half, o[1], o[0]), jnp.where(half, o[3], o[2])], axis=0).astype(bf16))

    def k_step(s0, k, mode, experts, pair, n_pair, low, high, blocks, shared=None):
        first = shared is None and n_pair == 3
        if first:
            own_to_sibling(k).wait_recv()
            hand_on(k).wait_recv()
        if shared is not None:
            x_copy(k, shared).wait_recv()

            @pl.when(shared == 0)
            def _():
                x_copy(k, 1).start()

        def put(jj, i, v):
            xg[2 * jj + i] = v
        gather(k, pair, n_pair, put)
        if first:
            def put_shared(jj, i, v):
                xy[(k * 2 + jj) * 2 + i] = v
            gather(k, 6, 2, put_shared)
        if first:
            x_copy(k, 0).start()

        for b, block in enumerate(blocks):
            for i in block:
                for m in range(2):
                    wait_up(slot_of(s0 + i, m))
            for i in block:
                two = shared is not None and i == len(experts) - 1
                lhs = jnp.concatenate([xy[(k * 2 + dp) * 2 + shared], xp[k, shared]], axis=0) if two else xg[i]
                rows = 2 * EROW if two else EROW
                for n in range(NF):
                    val = []
                    for m in range(2):
                        r = jnp.dot(lhs, ring[slot_of(s0 + i, m), n * KC:(n + 1) * KC, :], preferred_element_type=f32)
                        at = i * 2 * NF * EROW + (m * NF + n) * rows
                        if mode == "first":
                            acc[at:at + rows, :] = r
                        elif mode == "middle":
                            acc[at:at + rows, :] = acc[at:at + rows, :] + r
                        else:
                            val.append(acc[at:at + rows, :] + r)
                    if mode == "last":
                        a = (jax.nn.silu(val[0]) * val[1]).astype(bf16)
                        cols = slice(n * KC, (n + 1) * KC)
                        act[experts[i], :, cols] = a[:EROW]
                        if two:
                            xy[(n * 2 + dp) * 2 + shared] = a[EROW:]
                            a_copy(shared, n).start()
            for i in block:
                fill(s0 + i + AHEAD, low + i + AHEAD, high + i + AHEAD)
            if first and b == 0:
                if not isinstance(k, int) or k < NK - 1:
                    own_to_partner(k + 1).wait_recv()
                    hand_on(k + 1).start()

    def k_loop(base, per, low, high, **kw):
        k_step(base, 0, "first", low=low, high=high, **kw)

        def middle(k, _):
            k_step(base + k * per, k, "middle", low=low + per, high=high + 3 * per, **kw)
            return 0
        lax.fori_loop(1, NK - 1, middle, 0)
        k_step(base + (NK - 1) * per, NK - 1, "last", low=low + (NK - 1) * per, high=high + (NK - 1) * per, **kw)

    k_loop(0, G0, 0, 0, experts=tuple(range(G0)), pair=0, n_pair=3, blocks=((0, 1), (2, 3), (4, 5)))

    def shared_group(g, _):
        k_loop(S1 + g * (GS * NK), GS, S1, S1 + GS * NK, experts=(6 + 2 * g, 7 + 2 * g, 12 + 2 * dp + g),
               pair=3 + g, n_pair=1, blocks=((0, 1, 2),), shared=g)
        return 0
    lax.fori_loop(0, 2, shared_group, 0)
    build_combine()
    k_loop(S3, G3, S3, S3, experts=(10, 11), pair=5, n_pair=1, blocks=((0, 1),))
    for k in range(NK):
        for i in range(2):
            x_copy(k, i).wait_send()
    for i in range(2):
        for n in range(NF):
            a_copy(i, n).wait_send()

    def part_rows(c, where, which):
        return pl.ds(pl.multiple_of(((c % 2 * 2 + where) * 2 + which) * TOK, TOK), TOK)

    def cols_of(c):
        return pl.ds(c * WC, WC) if isinstance(c, int) else pl.ds(pl.multiple_of(c * WC, WC), WC)

    def s_copy(c, i):
        return pltpu.make_async_remote_copy(
            src_ref=acc.at[part_rows(c, i, 1 - core), pl.ds(0, WC)], dst_ref=sib.at[i, :, cols_of(c)],
            send_sem=s_send.at[c, i], recv_sem=s_recv.at[c, i], device_id={"ep": sibling}, device_id_type=MESH)

    def r_copy(c):
        return pltpu.make_async_remote_copy(
            src_ref=sib.at[0, :, cols_of(c)], dst_ref=rem.at[:, cols_of(c)],
            send_sem=r_send.at[c], recv_sem=r_recv.at[c], device_id={"ep": partner}, device_id_type=MESH)

    def relay(c):
        cols = cols_of(c)
        s_copy(c, 0).wait_recv()
        sib[0, :, cols] = sib[0, :, cols] + acc[part_rows(c, 0, core), 0:WC]
        r_copy(c).start()
        s_copy(c, 1).wait_recv()
        sib[1, :, cols] = sib[1, :, cols] + acc[part_rows(c, 1, core), 0:WC]

    def combine(c):
        @pl.when(c >= 2)
        def _():
            s_copy(c - 2, 0).wait_send()
            s_copy(c - 2, 1).wait_send()
        for i in range(2):
            ch = (1 - chip) if i == 0 else chip
            for w in range(2):
                d = ch * 2 + w
                rows = xy[pl.ds(d * (NE // 4), NE // 4), :, 0:WC].reshape(DSLOT, WC)
                tot = jnp.dot(cmb[d, 0], rows, preferred_element_type=f32)
                for q in range(1, 3):
                    tot = tot + jnp.dot(cmb[d, q], rows, preferred_element_type=f32)
                acc[part_rows(c, i, w), 0:WC] = tot
            s_copy(c, i).start()

    narrow = half[:, 0:WC]

    def trip(t, _):
        c, r = t // 2, t % 2
        s0 = P1 + 2 * t
        @pl.when(t == 1)
        def _():
            for i in range(2):
                for n in range(NF):
                    a_copy(i, n).wait_recv()
        for i in range(4):
            wait_up(slot_of(s0, i))
        for v in range(2):
            q = 2 * r + v
            ys = [jnp.dot(act[4 * q + i], ring[slot_of(s0 + v, i // 2), :, i % 2 * WC:(i % 2 + 1) * WC],
                          preferred_element_type=f32) for i in range(4)]
            for ch in range(2):
                r0, r1 = ch * PROW, (ch + 1) * PROW
                for w in range(2):
                    rows = [jnp.where(narrow, ys[2 * jj + w][r0:r1], ys[2 * jj + 1 - w][r0:r1]) for jj in range(2)]
                    xy[(2 * ch + w) * (NE // 4) + q, :, 0:WC] = jnp.concatenate(rows, axis=0).astype(bf16)

        @pl.when(t < P2 // 2 - AHEAD // 2)
        def _():
            for i in range(2):
                fill_down(s0 + i + AHEAD)

        @pl.when((r == 0) & (c > 1))
        def _():
            relay(c - 1)

        @pl.when(r == 1)
        def _():
            combine(c)

        @pl.when(t == 1)
        def _():
            relay(0)
        return 0

    lax.fori_loop(0, P2 // 2, trip, 0)
    relay(NC - 1)

    outs = []
    for c in range(NC):
        cols = cols_of(c)
        r_copy(c).wait_recv()
        xv[:, cols] = (xv[:, cols].astype(f32) + (sib[1, :, cols] + rem[:, cols])).astype(bf16)
        outs.append(pltpu.make_async_copy(xv.at[:, cols], out_hbm.at[:, cols], out_sem.at[c]))
        outs[-1].start()

    for k in range(NK):
        own_to_sibling(k).wait_send()
        own_to_partner(k).wait_send()
        hand_on(k).wait_send()
    for idx in range(3):
        pos_copy(idx).wait_send()
        gate_copy(idx).wait_send()
    for c in range(NC):
        r_copy(c).wait_send()
    for c in range(NC - 2, NC):
        for i in range(2):
            s_copy(c, i).wait_send()
    for o in outs:
        o.wait()


def solution(mesh):
    def local_block(x_in, norm_gain, w_router, expert_ids, w_gate, w_up, w_down):
        tokens, hidden = x_in.shape
        dma = pltpu.SemaphoreType.DMA
        return pl.pallas_call(
            kernel,
            out_shape=jax.ShapeDtypeStruct((tokens, hidden), bf16),
            in_specs=[pl.BlockSpec(memory_space=pl.ANY)] * 7,
            out_specs=pl.BlockSpec(memory_space=pl.ANY),
            scratch_shapes=[
                pltpu.VMEM((TOK, NK * KC), bf16),
                pltpu.VMEM((NK * KC // 128, 128), bf16),
                pltpu.VMEM((64, NK * KC), bf16),
                pltpu.VMEM((6, TOK), i32),
                pltpu.VMEM((NK, 4 * PAD, KC), bf16),
                pltpu.VMEM((4, NE, PAD), f32),
                pltpu.VMEM((4, NE, PAD), f32),
                pltpu.VMEM((4, NE, PAD), f32),
                pltpu.VMEM((4, NE, PAD), f32),
                pltpu.VMEM((4, NE // 2, GROW, PAD), bf16),
                pltpu.VMEM((4, 3, TOK, DSLOT), bf16),
                pltpu.VMEM((G0 * 2 * NF * EROW, KC), f32),
                pltpu.VMEM((NE, EROW, FF), bf16),
                pltpu.VMEM((NSLOT, FF, KC), bf16),
                pltpu.VMEM((G0, EROW, KC), bf16),
                pltpu.VMEM((NK * 4, EROW, KC), bf16),
                pltpu.VMEM((NK, 2, EROW, KC), bf16),
                pltpu.VMEM((2, TOK, NK * KC), f32),
                pltpu.VMEM((TOK, NK * KC), f32),
                dma((4,)), dma((NC,)), dma((NSLOT,)),
                dma((NK, 3)), dma((NK, 3)),
                dma((3,)), dma((3,)), dma((3,)), dma((3,)),
                dma((NK, 2)), dma((NK, 2)), dma((2, NF)), dma((2, NF)),
                dma((NC, 2)), dma((NC, 2)), dma((NC,)), dma((NC,)),
            ],
            compiler_params=pltpu.CompilerParams(
                collective_id=0, has_side_effects=True, vmem_limit_bytes=67_043_328),
            name="moe_step",
        )(x_in, norm_gain.reshape(hidden // 128, 128), w_router.T, expert_ids.T, w_gate, w_up, w_down)

    tok_spec = P(("dp", "ep"), None)
    expert_spec = P("ep", None, None)
    return jax.shard_map(local_block, mesh=mesh, in_specs=(tok_spec, P(None), P(None, None), tok_spec, expert_spec, expert_spec, expert_spec), out_specs=tok_spec, check_vma=False)
```

profile of v0, /device:TPU:0, one launch (start us, length us, event | category | flops | bytes accessed | tf_op | source)
XLA Modules:
  0.0 128.9 jit_solution(14589730866230610933)
XLA Ops:
  0.0 126.6 %moe_step.1 = bf16[192,2560]{1,0:T(8,128)(2,1)} custom-call(bf16[192,2560]{1,0:T(8,128)(2,1)} %x_hbm.1, bf16[20,128]{1,0:T(8,128)(2,1)} %bitcast.5, bf16[64,2560]{1,0:T(8,128)(2,1)} %bitcast.3, s32[6,192]{1,0:T(8,128)} %bitcast.4, bf16[16,2560,1536]{2,1,0:T(8,128)(2,1)} %wg_hbm.1, bf16[16,2560,1536]{2,1,0:T(8,128)(2,1)} %wu_hbm.1, bf16[16,1536,2560]{2,1,0:T(8,128)(2,1)} %wd_hbm.1), custom_call_target="tpu_custom_call" | custom-call | tf_op jit(solution)/shard_map/moe_step/pallas_call | solution.py:439
  126.6 2.2 %copy.9 = bf16[192,2560]{1,0:T(8,128)(2,1)} copy(bf16[192,2560]{1,0:T(8,128)(2,1)} %moe_step.1) | data formatting | bytes 1966080
where the time goes:
time: 129 us
  Pallas kernels  127 us (98%)
  local copies, waits for them, and re-layouts  2.21 us (2%)
    pallas_call x1, Pallas kernels, local_block(): pl.pallas_call(kernel, out_shape=jax.ShapeDtypeStruct((tokens, hidden), b...  127 us

commit v1 on v0

--- a/solution.py
+++ b/solution.py
@@ -21,10 +21,11 @@
 NF = 3
 NSLOT = 16
 AHEAD = NSLOT // 2
-G0, GS, G3 = 6, 3, 2
+G0 = 6
 S1 = G0 * NK
-S3 = S1 + 2 * GS * NK
-P1 = S3 + G3 * NK
+S3 = S1 + 36
+P1 = S3 + 12
+KB = 2 * KC
 WC = 256
 NC = NK * KC // WC
 P2 = NC * NE // 4
@@ -32,9 +33,9 @@
 MESH = pl.DeviceIdType.MESH
 
 
-def kernel(x_hbm, gain_hbm, wr_hbm, ids_hbm, wg_hbm, wu_hbm, wd_hbm, out_hbm,
-           xv, gv, wrv, idv, h_all, pos_own, gate_own, pos_all, gate_all, gat, cmb, acc, act, ring, xg, xy, xp, sib, rem,
-           in_sem, out_sem, ring_sem, h_send, h_recv, p_send, p_recv, g_send, g_recv, x_send, x_recv, a_send, a_recv,
+def kernel(x_hbm, gain_hbm, wr_hbm, ids_hbm, wg_hbm, wu_hbm, wd_hbm, xv,
+           gv, idv, h_all, pos_own, gate_own, pos_all, gate_all, gat, cmb, acc, act, ring, xg, xy, xp, sib, rem,
+           in_sem, ring_sem, h_send, h_recv, p_send, p_recv, g_send, g_recv, x_send, x_recv, a_send, a_recv,
            s_send, s_recv, r_send, r_recv):
     me = lax.axis_index("ep")
     dp = lax.axis_index("dp")
@@ -47,8 +48,10 @@
     twin = {"dp": 1 - dp, "ep": me}
 
     ins = [pltpu.make_async_copy(s, d, in_sem.at[i]) for i, (s, d) in enumerate(
-        ((ids_hbm, idv), (x_hbm, xv), (gain_hbm, gv), (wr_hbm, wrv)))]
-    for i in (1, 2, 0, 3):
+        ((ids_hbm, idv), (x_hbm, xv), (gain_hbm, gv)))]
+    ins += [pltpu.make_async_copy(wr_hbm.at[:, pl.ds(k * KC, KC)], xy.at[k, pl.ds(0, 64)], in_sem.at[3 + k])
+            for k in range(NK)]
+    for i in (1, 2, 0, 3, 4, 5, 6, 7):
         ins[i].start()
 
     def slot_of(s, i):
@@ -64,14 +67,24 @@
     def fill_first(s):
         fill_up(s, s % G0, s // G0)
 
-    def fill_shared(s):
-        t = s - S1
-        g, u = t // (GS * NK), t % (GS * NK)
-        i = u % GS
-        fill_up(s, 6 + 2 * g + i + i // 2 * (4 - g + 2 * dp), u // GS)
-
-    def fill_last(s):
-        fill_up(s, 10 + (s - S3) % G3, (s - S3) // G3)
+    def fill_unit(s, e, n, part):
+        cols = pl.ds(pl.multiple_of(n * KC, KC), KC)
+        for m, w in enumerate((wg_hbm, wu_hbm)):
+            if part == 0:
+                pltpu.make_async_copy(
+                    w.at[e, pl.ds(0, FF), cols], ring.at[slot_of(s, m)], ring_sem.at[slot_of(s, m)]).start()
+            else:
+                pltpu.make_async_copy(w.at[e, pl.ds(FF, KB), cols], ring.at[slot_of(s, m), pl.ds(0, KB)],
+                                      ring_sem.at[slot_of(s, m)]).start()
+
+    def fill_shared(s, part):
+        u = (s - S1) // 2
+        g, i = u // 9, u // 3 % 3
+        fill_unit(s, 6 + 2 * g + i + i // 2 * (4 - g + 2 * dp), u % 3, part)
+
+    def fill_last(s, part):
+        u = (s - S3) // 2
+        fill_unit(s, 10 + u // 3, u % 3, part)
 
     def fill_down(s):
         p = s - P1
@@ -82,17 +95,19 @@
                 wd_hbm.at[4 * q + i, :, pl.ds(pl.multiple_of(c * WC, WC), WC)],
                 ring.at[slot, :, pl.ds(i % 2 * WC, WC)], ring_sem.at[slot]).start()
 
-    spans = [(0, S1, fill_first), (S1, S3, fill_shared), (S3, P1, fill_last), (P1, P1 + P2, fill_down)]
+    spans = [(0, S1, lambda s, part: fill_first(s)), (S1, S3, fill_shared), (S3, P1, fill_last),
+             (P1, P1 + P2, lambda s, part: fill_down(s))]
 
     def fill(s, low, high):
+        part = low % 2
         todo = [v for v in spans if v[0] <= high and low < v[1]]
         for a, b, fn in todo:
             if a <= low and high < b:
-                fn(s)
+                fn(s, part)
             elif b <= low or high < a:
                 pass
             else:
-                pl.when((s >= a) & (s < b))(lambda fn=fn: fn(s))
+                pl.when((s >= a) & (s < b))(lambda fn=fn: fn(s, part))
 
     def wait_up(slot):
         pltpu.make_async_copy(wd_hbm.at[0, :, pl.ds(0, KC)], ring.at[slot], ring_sem.at[slot]).wait()
@@ -103,8 +118,6 @@
     pl.semaphore_signal(barrier, inc=1, device_id=twin, device_id_type=MESH)
 
     for d in range(4):
-        h_all[:, d * PAD + TOK:(d + 1) * PAD, :] = jnp.zeros((NK, PAD - TOK, KC), bf16)
-    for d in range(4):
         pos_own[d] = jnp.full((NE, PAD), MISS, f32)
         gate_own[d] = jnp.zeros((NE, PAD), f32)
 
@@ -112,7 +125,7 @@
         c.wait()
     for s in range(AHEAD):
         fill(s, s, s)
-    my_rows = pl.ds(pl.multiple_of(me * PAD, PAD), TOK)
+    my_rows = pl.ds(pl.multiple_of(me * TOK, TOK), TOK)
     ssq = jnp.zeros((TOK, 1), f32)
     for k in range(NK):
         xc = xv[:, k * KC:(k + 1) * KC].astype(f32)
@@ -138,7 +151,7 @@
         return small_copy(gate_own, gate_all, g_send, g_recv, idx)
 
     def h_copy(k, owner, target, ss):
-        rows = pl.ds(pl.multiple_of(owner * PAD, PAD), TOK)
+        rows = pl.ds(pl.multiple_of(owner * TOK, TOK), TOK)
         return pltpu.make_async_remote_copy(
             src_ref=h_all.at[k, rows], dst_ref=h_all.at[k, rows], send_sem=h_send.at[k, ss], recv_sem=h_recv.at[k, ss],
             device_id={"ep": target}, device_id_type=MESH)
@@ -159,7 +172,7 @@
 
     def a_copy(i, n):
         return pltpu.make_async_remote_copy(
-            src_ref=xy.at[(n * 2 + dp) * 2 + i], dst_ref=act.at[12 + 2 * dp + i, :, pl.ds(n * KC, KC)],
+            src_ref=xy.at[(n * 2 + 1 - dp) * 2 + i], dst_ref=act.at[12 + 2 * dp + i, :, pl.ds(n * KC, KC)],
             send_sem=a_send.at[i, n], recv_sem=a_recv.at[i, n], device_id=twin, device_id_type=MESH)
 
     own_to_partner(0).start()
@@ -181,11 +194,12 @@
         own_to_partner(k).start()
         own_to_sibling(k).start()
 
-    ins[3].wait()
+    for c in ins[3:]:
+        c.wait()
     logits = jnp.zeros((64, TOK), f32)
     for k in range(NK):
         logits = logits + lax.dot_general(
-            wrv[:, k * KC:(k + 1) * KC], h_all[k, my_rows, :], (((1,), (1,)), ((), ())), preferred_element_type=f32)
+            xy[k, 0:64, :], h_all[k, my_rows, :], (((1,), (1,)), ((), ())), preferred_element_type=f32)
     ex = jnp.exp(logits - jnp.max(logits, axis=0, keepdims=True))
     prob = ex / jnp.sum(ex, axis=0, keepdims=True)
     picked = prob * hit
@@ -210,7 +224,7 @@
         for j in range(NE // 2):
             ea, eb = 2 * j + d % 2, 2 * j + 1 - d % 2
             want = jnp.where(low, pos_all[d, ea:ea + 1, :], pos_all[d, eb:eb + 1, :] + CAP)
-            gat[d, j] = jnp.where(r_iota == want, 1.0, 0.0).astype(bf16)
+            gat[d, j] = jnp.where(r_iota == want, 1.0, 0.0)[:, :TOK].astype(bf16)
 
     def build_combine():
         for idx in range(3):
@@ -236,8 +250,8 @@
     half = lax.broadcasted_iota(i32, (PROW, KC), 0) < CAP
 
     def gather(k, pair, n_pair, store):
-        outs = [jnp.dot(gat[d, pl.ds(pair, n_pair)].reshape(n_pair * GROW, PAD),
-                        h_all[k, d * PAD:(d + 1) * PAD, :], preferred_element_type=f32) for d in range(4)]
+        outs = [jnp.dot(gat[d, pl.ds(pair, n_pair)].reshape(n_pair * GROW, TOK),
+                        h_all[k, d * TOK:(d + 1) * TOK, :], preferred_element_type=f32) for d in range(4)]
         for jj in range(n_pair):
             o = [v[jj * GROW:jj * GROW + PROW] for v in outs]
             store(jj, 0, jnp.concatenate(
@@ -245,80 +259,116 @@
             store(jj, 1, jnp.concatenate(
                 [jnp.where(half, o[1], o[0]), jnp.where(half, o[3], o[2])], axis=0).astype(bf16))
 
-    def k_step(s0, k, mode, experts, pair, n_pair, low, high, blocks, shared=None):
-        first = shared is None and n_pair == 3
-        if first:
-            own_to_sibling(k).wait_recv()
-            hand_on(k).wait_recv()
-        if shared is not None:
-            x_copy(k, shared).wait_recv()
-
-            @pl.when(shared == 0)
-            def _():
-                x_copy(k, 1).start()
-
+    def k_step(k, mode):
+        s0 = k * G0
+        low, high = (s0, s0) if isinstance(k, int) else (G0, 3 * G0)
+        own_to_sibling(k).wait_recv()
+        hand_on(k).wait_recv()
         def put(jj, i, v):
             xg[2 * jj + i] = v
-        gather(k, pair, n_pair, put)
-        if first:
-            def put_shared(jj, i, v):
-                xy[(k * 2 + jj) * 2 + i] = v
-            gather(k, 6, 2, put_shared)
-        if first:
-            x_copy(k, 0).start()
-
-        for b, block in enumerate(blocks):
+        gather(k, 0, 3, put)
+
+        def put_shared(jj, i, v):
+            xy[(k * 2 + jj) * 2 + i] = v
+        gather(k, 6, 2, put_shared)
+        x_copy(k, 0).start()
+
+        for b in range(G0 // 2):
+            block = (2 * b, 2 * b + 1)
             for i in block:
                 for m in range(2):
                     wait_up(slot_of(s0 + i, m))
             for i in block:
-                two = shared is not None and i == len(experts) - 1
-                lhs = jnp.concatenate([xy[(k * 2 + dp) * 2 + shared], xp[k, shared]], axis=0) if two else xg[i]
-                rows = 2 * EROW if two else EROW
                 for n in range(NF):
                     val = []
                     for m in range(2):
-                        r = jnp.dot(lhs, ring[slot_of(s0 + i, m), n * KC:(n + 1) * KC, :], preferred_element_type=f32)
-                        at = i * 2 * NF * EROW + (m * NF + n) * rows
+                        r = jnp.dot(xg[i], ring[slot_of(s0 + i, m), n * KC:(n + 1) * KC, :], preferred_element_type=f32)
+                        at = ((i * 2 + m) * NF + n) * EROW
                         if mode == "first":
-                            acc[at:at + rows, :] = r
+                            acc[at:at + EROW, :] = r
                         elif mode == "middle":
-                            acc[at:at + rows, :] = acc[at:at + rows, :] + r
+                            acc[at:at + EROW, :] = acc[at:at + EROW, :] + r
                         else:
-                            val.append(acc[at:at + rows, :] + r)
+                            val.append(acc[at:at + EROW, :] + r)
                     if mode == "last":
-                        a = (jax.nn.silu(val[0]) * val[1]).astype(bf16)
-                        cols = slice(n * KC, (n + 1) * KC)
-                        act[experts[i], :, cols] = a[:EROW]
-                        if two:
-                            xy[(n * 2 + dp) * 2 + shared] = a[EROW:]
-                            a_copy(shared, n).start()
+                        act[i, :, n * KC:(n + 1) * KC] = (jax.nn.silu(val[0]) * val[1]).astype(bf16)
             for i in block:
                 fill(s0 + i + AHEAD, low + i + AHEAD, high + i + AHEAD)
-            if first and b == 0:
+            if b == (G0 // 2 - 1 if mode == "first" else 0):
                 if not isinstance(k, int) or k < NK - 1:
                     own_to_partner(k + 1).wait_recv()
                     hand_on(k + 1).start()
 
-    def k_loop(base, per, low, high, **kw):
-        k_step(base, 0, "first", low=low, high=high, **kw)
-
-        def middle(k, _):
-            k_step(base + k * per, k, "middle", low=low + per, high=high + 3 * per, **kw)
+    k_step(0, "first")
+
+    def middle(k, _):
+        k_step(k, "middle")
+        return 0
+    lax.fori_loop(1, NK - 1, middle, 0)
+    k_step(NK - 1, "last")
+
+    def gather_pair(pair):
+        for k in range(NK):
+            def put(jj, i, v):
+                xg[NK * i + k] = v
+            gather(k, pair, 1, put)
+
+    def unit(s0, n, low, high, rows_of, store):
+        for m in range(2):
+            wait_up(slot_of(s0, m))
+        for m in range(2):
+            slot = slot_of(s0 + 1, m)
+            pltpu.make_async_copy(wg_hbm.at[0, pl.ds(FF, KB), pl.ds(0, KC)], ring.at[slot, pl.ds(0, KB)],
+                                  ring_sem.at[slot]).wait()
+        lhs_a = jnp.concatenate([rows_of(k) for k in range(3)], axis=1)
+        lhs_b = jnp.concatenate([rows_of(k) for k in range(3, NK)], axis=1)
+        val = [jnp.dot(lhs_a, ring[slot_of(s0, m)], preferred_element_type=f32)
+               + jnp.dot(lhs_b, ring[slot_of(s0 + 1, m), 0:KB, :], preferred_element_type=f32) for m in range(2)]
+        store(n, (jax.nn.silu(val[0]) * val[1]).astype(bf16))
+        for part in range(2):
+            fill(s0 + part + AHEAD, low + part + AHEAD, high + part + AHEAD)
+
+    def cols_ff(n):
+        return pl.ds(pl.multiple_of(n * KC, KC), KC)
+
+    def two_experts(base, e, low, high):
+        def body(u, _):
+            i, n = u // 3, u % 3
+
+            def store(n, a):
+                act[e + i, :, cols_ff(n)] = a
+            unit(base + 2 * u, n, low, high, lambda k: xg[NK * i + k], store)
             return 0
-        lax.fori_loop(1, NK - 1, middle, 0)
-        k_step(base + (NK - 1) * per, NK - 1, "last", low=low + (NK - 1) * per, high=high + (NK - 1) * per, **kw)
-
-    k_loop(0, G0, 0, 0, experts=tuple(range(G0)), pair=0, n_pair=3, blocks=((0, 1), (2, 3), (4, 5)))
+        lax.fori_loop(0, 6, body, 0)
 
     def shared_group(g, _):
-        k_loop(S1 + g * (GS * NK), GS, S1, S1 + GS * NK, experts=(6 + 2 * g, 7 + 2 * g, 12 + 2 * dp + g),
-               pair=3 + g, n_pair=1, blocks=((0, 1, 2),), shared=g)
+        gather_pair(3 + g)
+
+        @pl.when(g == 0)
+        def _():
+            for k in range(NK):
+                x_copy(k, 1).start()
+        two_experts(S1 + 18 * g, 6 + 2 * g, S1, S1 + 28)
+        for k in range(NK):
+            x_copy(k, g).wait_recv()
+        for n in range(NF):
+            x_copy(n, g).wait_send()
+
+        def body(n, _):
+            def store(n, a):
+                act[12 + 2 * dp + g, :, cols_ff(n)] = a[:EROW]
+                xy[(n * 2 + 1 - dp) * 2 + g] = a[EROW:]
+                a_copy(g, n).start()
+            unit(S1 + 18 * g + 12 + 2 * n, n, S1 + 12, S1 + 34,
+                 lambda k: jnp.concatenate([xy[(k * 2 + dp) * 2 + g], xp[k, g]], axis=0), store)
+            return 0
+        lax.fori_loop(0, NF, body, 0)
         return 0
     lax.fori_loop(0, 2, shared_group, 0)
     build_combine()
-    k_loop(S3, G3, S3, S3, experts=(10, 11), pair=5, n_pair=1, blocks=((0, 1),))
-    for k in range(NK):
+    gather_pair(5)
+    two_experts(S3, 10, S3, S3 + 10)
+    for k in range(NF, NK):
         for i in range(2):
             x_copy(k, i).wait_send()
     for i in range(2):
@@ -408,13 +458,10 @@
     lax.fori_loop(0, P2 // 2, trip, 0)
     relay(NC - 1)
 
-    outs = []
     for c in range(NC):
         cols = cols_of(c)
         r_copy(c).wait_recv()
         xv[:, cols] = (xv[:, cols].astype(f32) + (sib[1, :, cols] + rem[:, cols])).astype(bf16)
-        outs.append(pltpu.make_async_copy(xv.at[:, cols], out_hbm.at[:, cols], out_sem.at[c]))
-        outs[-1].start()
 
     for k in range(NK):
         own_to_sibling(k).wait_send()
@@ -428,8 +475,6 @@
     for c in range(NC - 2, NC):
         for i in range(2):
             s_copy(c, i).wait_send()
-    for o in outs:
-        o.wait()
 
 
 def solution(mesh):
@@ -438,37 +483,35 @@
         dma = pltpu.SemaphoreType.DMA
         return pl.pallas_call(
             kernel,
-            out_shape=jax.ShapeDtypeStruct((tokens, hidden), bf16),
+            out_shape=pltpu.VMEM((tokens, hidden), bf16),
             in_specs=[pl.BlockSpec(memory_space=pl.ANY)] * 7,
-            out_specs=pl.BlockSpec(memory_space=pl.ANY),
+            out_specs=pl.BlockSpec(memory_space=pltpu.VMEM),
             scratch_shapes=[
-                pltpu.VMEM((TOK, NK * KC), bf16),
                 pltpu.VMEM((NK * KC // 128, 128), bf16),
-                pltpu.VMEM((64, NK * KC), bf16),
                 pltpu.VMEM((6, TOK), i32),
-                pltpu.VMEM((NK, 4 * PAD, KC), bf16),
+                pltpu.VMEM((NK, 4 * TOK, KC), bf16),
                 pltpu.VMEM((4, NE, PAD), f32),
                 pltpu.VMEM((4, NE, PAD), f32),
                 pltpu.VMEM((4, NE, PAD), f32),
                 pltpu.VMEM((4, NE, PAD), f32),
-                pltpu.VMEM((4, NE // 2, GROW, PAD), bf16),
+                pltpu.VMEM((4, NE // 2, GROW, TOK), bf16),
                 pltpu.VMEM((4, 3, TOK, DSLOT), bf16),
                 pltpu.VMEM((G0 * 2 * NF * EROW, KC), f32),
                 pltpu.VMEM((NE, EROW, FF), bf16),
                 pltpu.VMEM((NSLOT, FF, KC), bf16),
-                pltpu.VMEM((G0, EROW, KC), bf16),
+                pltpu.VMEM((2 * NK, EROW, KC), bf16),
                 pltpu.VMEM((NK * 4, EROW, KC), bf16),
                 pltpu.VMEM((NK, 2, EROW, KC), bf16),
                 pltpu.VMEM((2, TOK, NK * KC), f32),
                 pltpu.VMEM((TOK, NK * KC), f32),
-                dma((4,)), dma((NC,)), dma((NSLOT,)),
+                dma((3 + NK,)), dma((NSLOT,)),
                 dma((NK, 3)), dma((NK, 3)),
                 dma((3,)), dma((3,)), dma((3,)), dma((3,)),
                 dma((NK, 2)), dma((NK, 2)), dma((2, NF)), dma((2, NF)),
                 dma((NC, 2)), dma((NC, 2)), dma((NC,)), dma((NC,)),
             ],
             compiler_params=pltpu.CompilerParams(
-                collective_id=0, has_side_effects=True, vmem_limit_bytes=67_043_328),
+                collective_id=0, has_side_effects=True, vmem_limit_bytes=66_060_288),
             name="moe_step",
         )(x_in, norm_gain.reshape(hidden // 128, 128), w_router.T, expert_ids.T, w_gate, w_up, w_down)
 

time: 129 us -> 126 us (0.977)
  Pallas kernels: 127 us -> 125 us
    pallas_call x1, Pallas kernels: 127 us -> 125 us  [local_block(): pl.pallas_call(kernel, out_shape=pltpu.VMEM((tokens, hidden), bf16), in_s...]
where the time goes in v1:
time: 126 us
  Pallas kernels  125 us (99%)
    pallas_call x1, Pallas kernels, local_block(): pl.pallas_call(kernel, out_shape=pltpu.VMEM((tokens, hidden), bf16), in_s...  125 us

profile of v1, /device:TPU:0, one launch (start us, length us, event | category | flops | bytes accessed | tf_op | source)
XLA Modules:
  0.0 125.9 jit_solution(1040186129227927818)
XLA Ops:
  0.0 125.0 %moe_step.1 = bf16[192,2560]{1,0:T(8,128)(2,1)S(1)} custom-call(bf16[192,2560]{1,0:T(8,128)(2,1)} %x_hbm.1, bf16[20,128]{1,0:T(8,128)(2,1)} %bitcast.5, bf16[64,2560]{1,0:T(8,128)(2,1)} %bitcast.3, s32[6,192]{1,0:T(8,128)} %bitcast.4, bf16[16,2560,1536]{2,1,0:T(8,128)(2,1)} %wg_hbm.1, bf16[16,2560,1536]{2,1,0:T(8,128)(2,1)} %wu_hbm.1, ...), custom_call_target="tpu_custom_call" | custom-call | tf_op jit(solution)/shard_map/moe_step/pallas_call | solution.py:484
  125.0 0.9 copy.9

commit v2 on v1

--- a/solution.py
+++ b/solution.py
@@ -231,21 +231,23 @@
             gate_copy(idx).wait_recv()
         le = lax.broadcasted_iota(i32, (NE, DSLOT), 1)
         ee = lax.broadcasted_iota(i32, (NE, DSLOT), 0)
-        lane = lax.broadcasted_iota(i32, (TOK, DSLOT), 1) % PROW
+        lane = lax.broadcasted_iota(i32, (48, DSLOT), 1) % PROW
         slot_r = jnp.where(lane < CAP, lane, lane - CAP).astype(f32)
         for d in range(4):
             swap = jnp.where(le % PROW < CAP, d % 2, 1 - d % 2)
             expand = (le // PROW * 2 + swap == ee).astype(f32).astype(bf16)
             ptok = jnp.transpose(pos_all[d])[:TOK]
             wtok = jnp.transpose(gate_all[d])[:TOK]
-            pexp = jnp.dot(ptok.astype(bf16), expand, preferred_element_type=f32)
-            sel = pexp == slot_r
-            rest = wtok
-            for i in range(3):
-                part = rest.astype(bf16)
-                rest = rest - part.astype(f32)
-                wexp = jnp.dot(part, expand, preferred_element_type=f32)
-                cmb[d, i] = jnp.where(sel, wexp, 0.0).astype(bf16)
+            for t in range(0, TOK, 48):
+                pexp = jnp.dot(ptok[t:t + 48].astype(bf16), expand, preferred_element_type=f32)
+                sel = pexp == slot_r
+                rest = wtok[t:t + 48]
+                parts = []
+                for i in range(3):
+                    part = rest.astype(bf16)
+                    rest = rest - part.astype(f32)
+                    parts.append(jnp.where(sel, jnp.dot(part, expand, preferred_element_type=f32), 0.0))
+                cmb[d, t:t + 48, :] = jnp.concatenate(parts, axis=1).astype(bf16)
 
     half = lax.broadcasted_iota(i32, (PROW, KC), 0) < CAP
 
@@ -396,6 +398,9 @@
         s_copy(c, 0).wait_recv()
         sib[0, :, cols] = sib[0, :, cols] + acc[part_rows(c, 0, core), 0:WC]
         r_copy(c).start()
+
+    def settle(c):
+        cols = cols_of(c)
         s_copy(c, 1).wait_recv()
         sib[1, :, cols] = sib[1, :, cols] + acc[part_rows(c, 1, core), 0:WC]
 
@@ -409,10 +414,8 @@
             for w in range(2):
                 d = ch * 2 + w
                 rows = xy[pl.ds(d * (NE // 4), NE // 4), :, 0:WC].reshape(DSLOT, WC)
-                tot = jnp.dot(cmb[d, 0], rows, preferred_element_type=f32)
-                for q in range(1, 3):
-                    tot = tot + jnp.dot(cmb[d, q], rows, preferred_element_type=f32)
-                acc[part_rows(c, i, w), 0:WC] = tot
+                acc[part_rows(c, i, w), 0:WC] = jnp.dot(
+                    cmb[d], jnp.concatenate([rows] * 3, axis=0), preferred_element_type=f32)
             s_copy(c, i).start()
 
     narrow = half[:, 0:WC]
@@ -442,21 +445,18 @@
             for i in range(2):
                 fill_down(s0 + i + AHEAD)
 
-        @pl.when((r == 0) & (c > 1))
+        @pl.when((r == 0) & (c > 0))
         def _():
-            relay(c - 1)
+            settle(c - 1)
 
         @pl.when(r == 1)
         def _():
             combine(c)
-
-        @pl.when(t == 1)
-        def _():
-            relay(0)
+            relay(c)
         return 0
 
     lax.fori_loop(0, P2 // 2, trip, 0)
-    relay(NC - 1)
+    settle(NC - 1)
 
     for c in range(NC):
         cols = cols_of(c)
@@ -495,7 +495,7 @@
                 pltpu.VMEM((4, NE, PAD), f32),
                 pltpu.VMEM((4, NE, PAD), f32),
                 pltpu.VMEM((4, NE // 2, GROW, TOK), bf16),
-                pltpu.VMEM((4, 3, TOK, DSLOT), bf16),
+                pltpu.VMEM((4, TOK, 3 * DSLOT), bf16),
                 pltpu.VMEM((G0 * 2 * NF * EROW, KC), f32),
                 pltpu.VMEM((NE, EROW, FF), bf16),
                 pltpu.VMEM((NSLOT, FF, KC), bf16),

time: 126 us -> 125 us (level)
  no operation moved by 1% of the time
where the time goes in v2:
time: 125 us
  Pallas kernels  124 us (99%)
    pallas_call x1, Pallas kernels, local_block(): pl.pallas_call(kernel, out_shape=pltpu.VMEM((tokens, hidden), bf16), in_s...  124 us

profile of v2, /device:TPU:0, one launch (start us, length us, event | category | flops | bytes accessed | tf_op | source)
XLA Modules:
  0.0 124.8 jit_solution(7237089049189725796)
XLA Ops:
  0.0 123.8 %moe_step.1 = bf16[192,2560]{1,0:T(8,128)(2,1)S(1)} custom-call(bf16[192,2560]{1,0:T(8,128)(2,1)} %x_hbm.1, bf16[20,128]{1,0:T(8,128)(2,1)} %bitcast.5, bf16[64,2560]{1,0:T(8,128)(2,1)} %bitcast.3, s32[6,192]{1,0:T(8,128)} %bitcast.4, bf16[16,2560,1536]{2,1,0:T(8,128)(2,1)} %wg_hbm.1, bf16[16,2560,1536]{2,1,0:T(8,128)(2,1)} %wu_hbm.1, ...), custom_call_target="tpu_custom_call" | custom-call | tf_op jit(solution)/shard_map/moe_step/pallas_call | solution.py:484
  123.8 0.9 copy.9
